TPU v7x, 32 devices: a whole 2x2x4 slice. The times are simulated.
32 devices in a mesh: groups: 2 (over y), seq: 4 (over z), head: 2 (over x), inner: 2 (over core).
Axes of the slice: x: 2, y: 2, z: 4, core: 2. Of those that a mesh axis runs over, the one named last changes fastest.
Arguments:
- queries: bfloat16 [4096, 2, 8, 128], P(('groups', 'seq'), 'head', 'inner'), parts along dimension 0, may hold values from -120 to 120
- grad_out: bfloat16 [4096, 2, 8, 128], P(('groups', 'seq'), 'head', 'inner'), parts along dimension 0, may hold values from -6 to 6
- keys: bfloat16 [4096, 2, 128], P(('groups', 'seq'), 'head'), parts along dimension 0, may hold values from -6 to 6
- values: bfloat16 [4096, 2, 128], P(('groups', 'seq'), 'head'), parts along dimension 0, may hold values from -6 to 6
- indices: int32 [2, 64, 16], P('head', 'groups'), parts along dimension 1, may hold values from 0 to 31, as said below
- valid: int32 [2, 64, 16], P('head', 'groups'), parts along dimension 1, may hold values from 0 to 1
Outputs:
- grad_queries: bfloat16 [4096, 2, 8, 128], P(('groups', 'seq'), 'head', 'inner'), parts along dimension 0
- grad_keys: bfloat16 [4096, 2, 128], P(('groups', 'seq'), 'head'), parts along dimension 0
- grad_values: bfloat16 [4096, 2, 128], P(('groups', 'seq'), 'head'), parts along dimension 0
There are 2 independent parts, one for each index of `groups`. A program takes and returns all parts, laid end to end along the dimension named above; each array names one. Nothing has to cross between parts.
Inputs may be any that keep to these rules, and one draw needn't show every extreme that they name: `indices`: call blocks r * 8 to r * 8 + 7 run r. For every KV head and query block b: slot 0 names b and is valid; the valid slots name distinct blocks at most b; over all query blocks of run r, the valid slots name blocks of runs later than r never, and for each earlier run exactly 4 distinct blocks of it. Slots that are not valid name arbitrary blocks.
All inputs are finite; a program needn't handle non-finite values.
Results may differ from a plain program's by a relative error of at most 0.007.
Values may be sent and summed in bfloat16 or wider, within the bound.
No kernel may reach another device: no remote copies, remote signals or barrier semaphores. Data moves between devices by JAX's collectives and lax.ppermute only.
A program may use at most 64 MiB of HBM per device.

v0:
```python
import math
import jax
import jax.numpy as jnp
from jax import lax
from jax.sharding import PartitionSpec as P

BLK = 64
TOPK = 16
CAP = 4


def per_device(queries, grad_out, keys, values, indices, valid):
    tokens = queries.shape[0]
    heads_here = queries.shape[2]
    width = queries.shape[3]
    seq_count = lax.axis_size("seq")
    seq_here = lax.axis_index("seq")
    blocks_here = tokens // BLK
    total_blocks = indices.shape[1]
    scaling = 1.0 / math.sqrt(width)
    remote_rows = seq_count * CAP
    dest_rows = remote_rows + blocks_here
    picks_all = indices[0]
    valid_all = valid[0] > 0
    owner_all = picks_all // blocks_here
    local_all = picks_all % blocks_here
    my_picks = lax.dynamic_slice_in_dim(picks_all, seq_here * blocks_here, blocks_here, 0)
    my_valid = lax.dynamic_slice_in_dim(valid_all, seq_here * blocks_here, blocks_here, 0)
    my_owner = my_picks // blocks_here
    my_local = my_picks % blocks_here
    remote = my_valid & (my_owner != seq_here)
    block_ids = jnp.arange(total_blocks, dtype=jnp.int32)
    hits_in = (my_picks[:, :, None] == block_ids[None, None, :]) & remote[:, :, None]
    present_in = jnp.any(hits_in, axis=(0, 1)).reshape(seq_count, blocks_here)
    rank_in = jnp.cumsum(present_in.astype(jnp.int32), axis=1) - 1
    slot_ref = jnp.sum(jnp.where(hits_in, rank_in.reshape(-1)[None, None, :], 0), axis=2)
    row_index = jnp.where(remote, my_owner * CAP + slot_ref, remote_rows + my_local)
    source_run = block_ids // blocks_here
    incoming = valid_all & (owner_all == seq_here) & (source_run != seq_here)[:, None]
    hits_out = (
        local_all[:, :, None] == jnp.arange(blocks_here, dtype=jnp.int32)[None, None, :]
    ) & incoming[:, :, None]
    present_out = jnp.any(hits_out.reshape(seq_count, blocks_here * TOPK, blocks_here), axis=1)
    rank_out = jnp.cumsum(present_out.astype(jnp.int32), axis=1) - 1
    choose_out = present_out[:, None, :] & (
        rank_out[:, None, :] == jnp.arange(CAP, dtype=jnp.int32)[None, :, None]
    )
    wanted = my_picks.reshape(-1)
    blank = jnp.zeros((blocks_here * TOPK, BLK, width), jnp.bfloat16)
    carry = (blank, blank)
    key_piece = lax.all_gather(keys, "seq", axis=0, tiled=True)
    value_piece = lax.all_gather(values, "seq", axis=0, tiled=True)
    count = key_piece.shape[0] // BLK
    relative = wanted
    inside = (relative >= 0) & (relative < count)
    relative = jnp.clip(relative, 0, count - 1)
    key_rows = jnp.take(key_piece[:, 0].reshape(count, BLK, width), relative, axis=0)
    value_rows = jnp.take(value_piece[:, 0].reshape(count, BLK, width), relative, axis=0)
    sel_keys = jnp.where(inside[:, None, None], key_rows, carry[0])
    sel_values = jnp.where(inside[:, None, None], value_rows, carry[1])
    group = math.gcd(blocks_here, max(1, 512 // (BLK * heads_here)))
    steps_count = blocks_here // group
    span = TOPK * BLK
    position = jnp.arange(BLK, dtype=jnp.int32)
    causal = position[None, :] <= position[:, None]
    block_global = seq_here * blocks_here + jnp.arange(blocks_here, dtype=jnp.int32)
    before = my_picks < block_global[:, None]
    same = my_picks == block_global[:, None]
    allowed = my_valid[:, None, :, None] & (
        before[:, None, :, None] | same[:, None, :, None] & causal[None, :, None, :]
    )
    allowed = allowed.reshape(steps_count, group, BLK, span)
    query_steps = queries[:, 0].reshape(steps_count, group, BLK, heads_here, width)
    grad_steps = grad_out[:, 0].reshape(steps_count, group, BLK, heads_here, width)
    key_steps = sel_keys.reshape(steps_count, group, span, width)
    value_steps = sel_values.reshape(steps_count, group, span, width)
    row_steps = row_index.reshape(steps_count, group * TOPK)

    def attend(carry, inputs):
        key_acc, value_acc = carry
        q_group, do_group, k_group, v_group, mask_group, rows_group = inputs
        mask_heads = mask_group[:, None, :, :]
        scores = (
            jnp.einsum("qigw,qsw->qgis", q_group, k_group, preferred_element_type=jnp.float32)
            * scaling
        )
        highest = jnp.max(jnp.where(mask_heads, scores, -jnp.inf), axis=-1, keepdims=True)
        weights = jnp.where(mask_heads, jnp.exp(scores - highest), 0.0)
        probs = weights / jnp.sum(weights, axis=-1, keepdims=True)
        probs_b = probs.astype(jnp.bfloat16)
        dprobs = jnp.einsum("qigw,qsw->qgis", do_group, v_group, preferred_element_type=jnp.float32)
        delta = jnp.sum(probs * dprobs, axis=-1, keepdims=True)
        dscores = (probs * (dprobs - delta)).astype(jnp.bfloat16)
        query_grad = (
            jnp.einsum("qgis,qsw->qigw", dscores, k_group, preferred_element_type=jnp.float32)
            * scaling
        ).astype(jnp.bfloat16)
        key_terms = (
            jnp.einsum("qgis,qigw->qsw", dscores, q_group, preferred_element_type=jnp.float32)
            * scaling
        )
        value_terms = jnp.einsum(
            "qgis,qigw->qsw", probs_b, do_group, preferred_element_type=jnp.float32
        )
        key_acc = key_acc.at[rows_group].add(key_terms.reshape(group * TOPK, BLK * width))
        value_acc = value_acc.at[rows_group].add(value_terms.reshape(group * TOPK, BLK * width))
        return ((key_acc, value_acc), query_grad)

    zeros_dest = jnp.zeros((dest_rows, BLK * width), jnp.float32)
    (key_acc, value_acc), query_grads = lax.scan(
        attend,
        (zeros_dest, zeros_dest),
        (query_steps, grad_steps, key_steps, value_steps, allowed, row_steps),
    )
    grad_queries = query_grads.reshape(tokens, 1, heads_here, width)
    send_key_tiles = key_acc[:remote_rows].reshape(seq_count, CAP, BLK * width)
    send_value_tiles = value_acc[:remote_rows].reshape(seq_count, CAP, BLK * width)
    own_keys = key_acc[remote_rows:]
    own_values = value_acc[remote_rows:]
    choose_float = choose_out.astype(jnp.float32)
    back_keys, back_values = (
        lax.all_to_all(send_key_tiles, "seq", split_axis=0, concat_axis=0, tiled=True),
        lax.all_to_all(send_value_tiles, "seq", split_axis=0, concat_axis=0, tiled=True),
    )
    local_keys = own_keys + jnp.einsum(
        "dcb,dcx->bx", choose_float, back_keys, precision=lax.Precision.HIGHEST
    )
    local_values = own_values + jnp.einsum(
        "dcb,dcx->bx", choose_float, back_values, precision=lax.Precision.HIGHEST
    )
    total_keys, total_values = lax.psum((local_keys, local_values), "inner")
    grad_keys = total_keys.astype(jnp.bfloat16).reshape(tokens, 1, width)
    grad_values = total_values.astype(jnp.bfloat16).reshape(tokens, 1, width)
    return (grad_queries, grad_keys, grad_values)


def solution(mesh):
    return jax.shard_map(
        per_device,
        mesh=mesh,
        in_specs=(
            P(("groups", "seq"), "head", "inner", None),
            P(("groups", "seq"), "head", "inner", None),
            P(("groups", "seq"), "head", None),
            P(("groups", "seq"), "head", None),
            P("head", "groups", None),
            P("head", "groups", None),
        ),
        out_specs=(
            P(("groups", "seq"), "head", "inner", None),
            P(("groups", "seq"), "head", None),
            P(("groups", "seq"), "head", None),
        ),
        check_vma=False,
    )
```

profile of v0, /device:TPU:0, one launch (start us, length us, event | category | flops | bytes accessed | tf_op | source)
XLA Modules:
  0.0 166.9 jit_solution(11409170172867323838)
XLA Ops:
  4.3 17.6 %all_gather.6 = bf16[2048,1,128]{2,0,1:T(8,128)(2,1)S(1)} all-gather(bf16[512,1,128]{2,0,1:T(8,128)(2,1)} %param.12), channel_id=1, replica_groups=mesh['groups'=2,'seq'=4,'head'=2,'inner'=2] {'seq'}, dimensions={0}, use_global_device_ids=true | all-gather | bytes 655360 | tf_op jit(solution)/shard_map/all_gather | solution.py:51
  21.9 16.6 %all_gather.7 = bf16[2048,1,128]{2,0,1:T(8,128)(2,1)S(1)} all-gather(bf16[512,1,128]{2,0,1:T(8,128)(2,1)} %param.13), channel_id=1, replica_groups=mesh['groups'=2,'seq'=4,'head'=2,'inner'=2] {'seq'}, dimensions={0}, use_global_device_ids=true | all-gather | bytes 655360 | tf_op jit(solution)/shard_map/all_gather | solution.py:52
  39.4 2.1 %gather_fusion = bf16[128,64,128]{2,1,0:T(8,128)(2,1)} fusion(bf16[32,64,128]{2,1,0:T(8,128)(2,1)S(1)} %bitcast.131, s32[1024]{0:T(1024)S(1)} %pad_clamp_fusion), kind=kCustom, calls=%fused_computation.clone | custom fusion | bytes 4194816 | tf_op jit(solution)/shard_map/jit(_take)/gather | solution.py:57
  42.8 3.7 %select_select_fusion = (bf16[128,64,128]{2,1,0:T(8,128)(2,1)}, bf16[128,64,128]{2,1,0:T(8,128)(2,1)}) fusion(bf16[128,64,128]{2,1,0:T(8,128)(2,1)S(1)} %gather_fusion.1, pred[128]{0:T(512)(128)(4,1)S(1)} %compare_and_fusion.2, pred[128]{0:T(512)(128)(4,1)S(1)} %and.166, bf16[128,64,128]{2,1,0:T(8,128)(2,1)} %gather_fusion), kind=kLoop, calls=%fused_computation.54 | loop fusion | flops 4194304 | bytes 8388864 | tf_op jit(solution)/shard_map/jit(_where)/select_n | solution.py:60
  46.6 84.0 %while.14 = (s32[]{:T(128)}, f32[24,8192]{1,0:T(8,128)S(1)}, f32[24,8192]{1,0:T(8,128)S(1)}, bf16[4,2,64,4,128]{4,3,2,1,0:T(4,128)(2,1)}, s32[4,32]{1,0:T(4,128)...) while((s32[]{:T(128)}, f32[24,8192]{1,0:T(8,128)S(1)}, ...), condition=%wide.region_9.11_spmd, body=%wide.region_3.10_spmd.sunk | while | flops 679871104 | bytes 52703944 | solution.py:110
  48.6 1.5 fusion.74
  50.9 1.3 copy-done
  52.2 1.7 %convolution_bitcast_fusion.5 = f32[2,1024,128]{2,1,0:T(8,128)} fusion(bf16[1,2,64,4,128]{4,3,2,1,0:T(4,128)(2,1)S(1)} %get-tuple-element.196, f32[2,4,64,1024]{3,2,1,0:T(8,128)S(1)} %get-tuple-element.194, f32[2,4,64]{2,1,0:T(4,128)S(1)} %get-tuple-element.195), kind=kOutput, calls=%fused_computation.16.clone.1 | convolution fusion | flops 135266304 | bytes 3278848 | tf_op jit(solution)/shard_map/while/body/eval_jaxpr/qgis,qigw->qsw/dot_general | solution.py:102
  53.9 1.4 reshape.340
  55.3 2.1 %scatter_fusion.1 = f32[24,8192]{1,0:T(8,128)S(1)} fusion(f32[24,8192]{1,0:T(8,128)S(1)} %get-tuple-element.212, s32[32]{0:T(128)S(1)} %fusion.73, f32[32,8192]{1,0:T(8,128)S(1)} %reshape.340), kind=kCustom, calls=%fused_computation.3.clone.1 | custom fusion | flops 262144 | bytes 3145856 | tf_op jit(solution)/shard_map/while/body/eval_jaxpr/scatter-add | solution.py:106
  57.4 2.4 %fusion.76 = (f32[2,4,64]{2,1,0:T(4,128)S(1)}, f32[2,1024,64,4]{1,2,3,0:T(8,128)S(1)}) fusion(f32[2,4,64,1024]{3,2,1,0:T(8,128)} %copy-done, f32[2,4,64]{2,1,0:T(4,128)S(1)} %get-tuple-element.195, bf16[1,2,64,4,128]{4,3,2,1,0:T(4,128)(2,1)S(1)} %get-tuple-element.196, bf16[4,2,1024,128]{3,2,1,0:T(8,128)(2,1)} %get-tuple-element.229, s32[]{:T(128)S(6)} %copy.84), kind=kOutput, calls=%fused_computation.7.clone.1 | convolution fusion | flops 135790080 | bytes 4853764 | tf_op jit(solution)/shard_map/while/body/eval_jaxpr/qigw,qsw->qgis/dot_general | solution.py:91
  60.2 1.5 fusion.79
  61.7 1.5 fusion.78
  63.3 1.4 reshape.339
  64.7 2.1 %scatter_fusion = f32[24,8192]{1,0:T(8,128)S(1)} fusion(f32[24,8192]{1,0:T(8,128)S(1)} %get-tuple-element.211, s32[32]{0:T(128)S(1)} %fusion.73, f32[32,8192]{1,0:T(8,128)S(1)} %reshape.339), kind=kCustom, calls=%fused_computation.2.clone.1 | custom fusion | flops 262144 | bytes 3145856 | tf_op jit(solution)/shard_map/while/body/eval_jaxpr/scatter-add | solution.py:105
  69.6 1.5 fusion.74
  71.9 1.3 copy-done
  73.2 1.7 %convolution_bitcast_fusion.5 = f32[2,1024,128]{2,1,0:T(8,128)} fusion(bf16[1,2,64,4,128]{4,3,2,1,0:T(4,128)(2,1)S(1)} %get-tuple-element.196, f32[2,4,64,1024]{3,2,1,0:T(8,128)S(1)} %get-tuple-element.194, f32[2,4,64]{2,1,0:T(4,128)S(1)} %get-tuple-element.195), kind=kOutput, calls=%fused_computation.16.clone.1 | convolution fusion | flops 135266304 | bytes 3278848 | tf_op jit(solution)/shard_map/while/body/eval_jaxpr/qgis,qigw->qsw/dot_general | solution.py:102
  74.9 1.4 reshape.340
  76.3 2.1 %scatter_fusion.1 = f32[24,8192]{1,0:T(8,128)S(1)} fusion(f32[24,8192]{1,0:T(8,128)S(1)} %get-tuple-element.212, s32[32]{0:T(128)S(1)} %fusion.73, f32[32,8192]{1,0:T(8,128)S(1)} %reshape.340), kind=kCustom, calls=%fused_computation.3.clone.1 | custom fusion | flops 262144 | bytes 3145856 | tf_op jit(solution)/shard_map/while/body/eval_jaxpr/scatter-add | solution.py:106
  78.4 2.4 %fusion.76 = (f32[2,4,64]{2,1,0:T(4,128)S(1)}, f32[2,1024,64,4]{1,2,3,0:T(8,128)S(1)}) fusion(f32[2,4,64,1024]{3,2,1,0:T(8,128)} %copy-done, f32[2,4,64]{2,1,0:T(4,128)S(1)} %get-tuple-element.195, bf16[1,2,64,4,128]{4,3,2,1,0:T(4,128)(2,1)S(1)} %get-tuple-element.196, bf16[4,2,1024,128]{3,2,1,0:T(8,128)(2,1)} %get-tuple-element.229, s32[]{:T(128)S(6)} %copy.84), kind=kOutput, calls=%fused_computation.7.clone.1 | convolution fusion | flops 135790080 | bytes 4853764 | tf_op jit(solution)/shard_map/while/body/eval_jaxpr/qigw,qsw->qgis/dot_general | solution.py:91
  81.2 1.5 fusion.79
  82.7 1.5 fusion.78
  84.3 1.4 reshape.339
  85.7 2.1 %scatter_fusion = f32[24,8192]{1,0:T(8,128)S(1)} fusion(f32[24,8192]{1,0:T(8,128)S(1)} %get-tuple-element.211, s32[32]{0:T(128)S(1)} %fusion.73, f32[32,8192]{1,0:T(8,128)S(1)} %reshape.339), kind=kCustom, calls=%fused_computation.2.clone.1 | custom fusion | flops 262144 | bytes 3145856 | tf_op jit(solution)/shard_map/while/body/eval_jaxpr/scatter-add | solution.py:105
  90.6 1.5 fusion.74
  94.2 1.7 %convolution_bitcast_fusion.5 = f32[2,1024,128]{2,1,0:T(8,128)} fusion(bf16[1,2,64,4,128]{4,3,2,1,0:T(4,128)(2,1)S(1)} %get-tuple-element.196, f32[2,4,64,1024]{3,2,1,0:T(8,128)S(1)} %get-tuple-element.194, f32[2,4,64]{2,1,0:T(4,128)S(1)} %get-tuple-element.195), kind=kOutput, calls=%fused_computation.16.clone.1 | convolution fusion | flops 135266304 | bytes 3278848 | tf_op jit(solution)/shard_map/while/body/eval_jaxpr/qgis,qigw->qsw/dot_general | solution.py:102
  95.9 1.4 reshape.340
  97.3 2.1 %scatter_fusion.1 = f32[24,8192]{1,0:T(8,128)S(1)} fusion(f32[24,8192]{1,0:T(8,128)S(1)} %get-tuple-element.212, s32[32]{0:T(128)S(1)} %fusion.73, f32[32,8192]{1,0:T(8,128)S(1)} %reshape.340), kind=kCustom, calls=%fused_computation.3.clone.1 | custom fusion | flops 262144 | bytes 3145856 | tf_op jit(solution)/shard_map/while/body/eval_jaxpr/scatter-add | solution.py:106
  99.4 2.4 %fusion.76 = (f32[2,4,64]{2,1,0:T(4,128)S(1)}, f32[2,1024,64,4]{1,2,3,0:T(8,128)S(1)}) fusion(f32[2,4,64,1024]{3,2,1,0:T(8,128)} %copy-done, f32[2,4,64]{2,1,0:T(4,128)S(1)} %get-tuple-element.195, bf16[1,2,64,4,128]{4,3,2,1,0:T(4,128)(2,1)S(1)} %get-tuple-element.196, bf16[4,2,1024,128]{3,2,1,0:T(8,128)(2,1)} %get-tuple-element.229, s32[]{:T(128)S(6)} %copy.84), kind=kOutput, calls=%fused_computation.7.clone.1 | convolution fusion | flops 135790080 | bytes 4853764 | tf_op jit(solution)/shard_map/while/body/eval_jaxpr/qigw,qsw->qgis/dot_general | solution.py:91
  102.2 1.5 fusion.79
  103.7 1.5 fusion.78
  105.3 1.4 reshape.339
  106.7 2.1 %scatter_fusion = f32[24,8192]{1,0:T(8,128)S(1)} fusion(f32[24,8192]{1,0:T(8,128)S(1)} %get-tuple-element.211, s32[32]{0:T(128)S(1)} %fusion.73, f32[32,8192]{1,0:T(8,128)S(1)} %reshape.339), kind=kCustom, calls=%fused_computation.2.clone.1 | custom fusion | flops 262144 | bytes 3145856 | tf_op jit(solution)/shard_map/while/body/eval_jaxpr/scatter-add | solution.py:105
  111.6 1.5 fusion.74
  115.2 1.7 %convolution_bitcast_fusion.5 = f32[2,1024,128]{2,1,0:T(8,128)} fusion(bf16[1,2,64,4,128]{4,3,2,1,0:T(4,128)(2,1)S(1)} %get-tuple-element.196, f32[2,4,64,1024]{3,2,1,0:T(8,128)S(1)} %get-tuple-element.194, f32[2,4,64]{2,1,0:T(4,128)S(1)} %get-tuple-element.195), kind=kOutput, calls=%fused_computation.16.clone.1 | convolution fusion | flops 135266304 | bytes 3278848 | tf_op jit(solution)/shard_map/while/body/eval_jaxpr/qgis,qigw->qsw/dot_general | solution.py:102
  116.9 1.4 reshape.340
  118.3 2.1 %scatter_fusion.1 = f32[24,8192]{1,0:T(8,128)S(1)} fusion(f32[24,8192]{1,0:T(8,128)S(1)} %get-tuple-element.212, s32[32]{0:T(128)S(1)} %fusion.73, f32[32,8192]{1,0:T(8,128)S(1)} %reshape.340), kind=kCustom, calls=%fused_computation.3.clone.1 | custom fusion | flops 262144 | bytes 3145856 | tf_op jit(solution)/shard_map/while/body/eval_jaxpr/scatter-add | solution.py:106
  120.4 2.4 %fusion.76 = (f32[2,4,64]{2,1,0:T(4,128)S(1)}, f32[2,1024,64,4]{1,2,3,0:T(8,128)S(1)}) fusion(f32[2,4,64,1024]{3,2,1,0:T(8,128)} %copy-done, f32[2,4,64]{2,1,0:T(4,128)S(1)} %get-tuple-element.195, bf16[1,2,64,4,128]{4,3,2,1,0:T(4,128)(2,1)S(1)} %get-tuple-element.196, bf16[4,2,1024,128]{3,2,1,0:T(8,128)(2,1)} %get-tuple-element.229, s32[]{:T(128)S(6)} %copy.84), kind=kOutput, calls=%fused_computation.7.clone.1 | convolution fusion | flops 135790080 | bytes 4853764 | tf_op jit(solution)/shard_map/while/body/eval_jaxpr/qigw,qsw->qgis/dot_general | solution.py:91
  123.2 1.5 fusion.79
  124.7 1.5 fusion.78
  126.3 1.4 reshape.339
  127.7 2.1 %scatter_fusion = f32[24,8192]{1,0:T(8,128)S(1)} fusion(f32[24,8192]{1,0:T(8,128)S(1)} %get-tuple-element.211, s32[32]{0:T(128)S(1)} %fusion.73, f32[32,8192]{1,0:T(8,128)S(1)} %reshape.339), kind=kCustom, calls=%fused_computation.2.clone.1 | custom fusion | flops 262144 | bytes 3145856 | tf_op jit(solution)/shard_map/while/body/eval_jaxpr/scatter-add | solution.py:105
  131.5 4.1 %all-to-all-start = ((f32[4,4,8192]{2,1,0:T(4,128)}), f32[4,4,8192]{2,1,0:T(4,128)S(1)}, u32[]{:S(2)}, u32[]{:S(2)}) async-start(f32[4,4,8192]{2,1,0:T(4,128)} %reshape.280), calls=%async_computation | async-start | bytes 1048576 | tf_op jit(solution)/shard_map/all_to_all | solution.py:122
  137.0 8.9 %all-to-all-done = f32[4,4,8192]{2,1,0:T(4,128)S(1)} async-done(((f32[4,4,8192]{2,1,0:T(4,128)}), f32[4,4,8192]{2,1,0:T(4,128)S(1)}, u32[]{:S(2)}, u32[]{:S(2)}) %all-to-all-start) | async-done | bytes 524320 | tf_op jit(solution)/shard_map/all_to_all | solution.py:122
  146.0 3.5 %all-to-all-start.1 = ((f32[4,4,8192]{2,1,0:T(4,128)}), f32[4,4,8192]{2,1,0:T(4,128)S(1)}, u32[]{:S(2)}, u32[]{:S(2)}) async-start(f32[4,4,8192]{2,1,0:T(4,128)} %reshape.282), calls=%async_computation.1 | async-start | bytes 1048576 | tf_op jit(solution)/shard_map/all_to_all | solution.py:123
  150.7 9.0 %all-to-all-done.1 = f32[4,4,8192]{2,1,0:T(4,128)S(1)} async-done(((f32[4,4,8192]{2,1,0:T(4,128)}), f32[4,4,8192]{2,1,0:T(4,128)S(1)}, u32[]{:S(2)}, u32[]{:S(2)}) %all-to-all-start.1) | async-done | bytes 524320 | tf_op jit(solution)/shard_map/all_to_all | solution.py:123
  160.6 4.8 %all-reduce.2 = (bf16[8,8192]{1,0:T(8,128)(2,1)S(1)}, bf16[8,8192]{1,0:T(8,128)(2,1)S(1)}) all-reduce(f32[8,8192]{1,0:T(8,128)S(1)} %fusion.30, f32[8,8192]{1,0:T(8,128)S(1)} %fusion.31), channel_id=1, replica_groups=mesh['groups'=2,'seq'=4,'head'=2,'inner'=2] {'inner'}, use_global_device_ids=true, to_apply=%region_12.14 | all-reduce | flops 131072 | bytes 786432 | tf_op jit(solution)/shard_map/psum | solution.py:131
  (93 shorter events, 30.2 us)
Async XLA Ops:
  50.9 1.3 copy-start
  57.4 2.4 %copy-start.1 = (f32[2,4,64,1024]{3,2,1,0:T(8,128)S(1)}, f32[2,4,64,1024]{3,2,1,0:T(8,128)}, u32[]{:S(2)}) copy-start(f32[2,4,64,1024]{3,2,1,0:T(8,128)} %copy-done) | copy-start | bytes 6291460 | tf_op jit(solution)/shard_map/while
  71.9 1.3 copy-start
  78.4 2.4 %copy-start.1 = (f32[2,4,64,1024]{3,2,1,0:T(8,128)S(1)}, f32[2,4,64,1024]{3,2,1,0:T(8,128)}, u32[]{:S(2)}) copy-start(f32[2,4,64,1024]{3,2,1,0:T(8,128)} %copy-done) | copy-start | bytes 6291460 | tf_op jit(solution)/shard_map/while
  92.9 1.3 copy-start
  99.4 2.4 %copy-start.1 = (f32[2,4,64,1024]{3,2,1,0:T(8,128)S(1)}, f32[2,4,64,1024]{3,2,1,0:T(8,128)}, u32[]{:S(2)}) copy-start(f32[2,4,64,1024]{3,2,1,0:T(8,128)} %copy-done) | copy-start | bytes 6291460 | tf_op jit(solution)/shard_map/while
  113.9 1.3 copy-start
  120.4 2.4 %copy-start.1 = (f32[2,4,64,1024]{3,2,1,0:T(8,128)S(1)}, f32[2,4,64,1024]{3,2,1,0:T(8,128)}, u32[]{:S(2)}) copy-start(f32[2,4,64,1024]{3,2,1,0:T(8,128)} %copy-done) | copy-start | bytes 6291460 | tf_op jit(solution)/shard_map/while
  131.5 14.4 %all-to-all-start = ((f32[4,4,8192]{2,1,0:T(4,128)}), f32[4,4,8192]{2,1,0:T(4,128)S(1)}, u32[]{:S(2)}, u32[]{:S(2)}) async-start(f32[4,4,8192]{2,1,0:T(4,128)} %reshape.280), calls=%async_computation | async-start | bytes 1048576 | tf_op jit(solution)/shard_map/all_to_all | solution.py:122
  146.0 13.7 %all-to-all-start.1 = ((f32[4,4,8192]{2,1,0:T(4,128)}), f32[4,4,8192]{2,1,0:T(4,128)S(1)}, u32[]{:S(2)}, u32[]{:S(2)}) async-start(f32[4,4,8192]{2,1,0:T(4,128)} %reshape.282), calls=%async_computation.1 | async-start | bytes 1048576 | tf_op jit(solution)/shard_map/all_to_all | solution.py:123
where the time goes:
time: 168 us; the launch traced here: 167 us
  blocking collectives  39 us (23%)
  local copies, waits for them, and re-layouts  37.2 us (22%)
  matrix products  36.2 us (22%)
  other arithmetic  27.9 us (17%)
  waiting for transfers between devices  17.9 us (11%)
  starting transfers between devices  7.61 us (5%)
    all_gather x1, blocking collectives, per_device(): key_piece = lax.all_gather(keys, 'seq', axis=0, tiled=True)  17.6 us
    all_gather x1, blocking collectives, per_device(): value_piece = lax.all_gather(values, 'seq', axis=0, tiled=True)  16.6 us
    dot_general x4, matrix products, attend(): jnp.einsum('qigw,qsw->qgis', do_group, v_group, preferred_element_type=jn...  9.67 us
    all_to_all x1, waiting for transfers between devices, per_device(): lax.all_to_all(send_value_tiles, 'seq', split_axis=0, concat_axis=0, tile...  9 us
    all_to_all x1, waiting for transfers between devices, per_device(): lax.all_to_all(send_key_tiles, 'seq', split_axis=0, concat_axis=0, tiled=...  8.93 us
    scatter-add x4, other arithmetic, attend(): key_acc.at[rows_group].add(key_terms.reshape(group * TOPK, BLK * width))  8.42 us
    scatter-add x4, other arithmetic, attend(): value_acc.at[rows_group].add(value_terms.reshape(group * TOPK, BLK * width))  8.42 us
    dot_general x4, matrix products, attend(): jnp.einsum('qgis,qigw->qsw', probs_b, do_group, preferred_element_type=jn...  6.69 us
  transfers between devices with their start and end apart: 2, of which 2 were waited for; matrix products, arithmetic and copies ran while one was open for 2% of the time, Pallas kernels for 0%

commit v1 on v0

--- a/solution.py
+++ b/solution.py
@@ -49,7 +49,12 @@
     blank = jnp.zeros((blocks_here * TOPK, BLK, width), jnp.bfloat16)
     carry = (blank, blank)
     key_piece = lax.all_gather(keys, "seq", axis=0, tiled=True)
-    value_piece = lax.all_gather(values, "seq", axis=0, tiled=True)
+    ring = [values]
+    for hop in range(3):
+        ring.append(lax.ppermute(ring[-1], "seq", [(dev, (dev + 1) % 4) for dev in range(4)]))
+    value_piece = jnp.roll(
+        jnp.concatenate(ring[::-1], axis=0), (lax.axis_index("seq") + 1) * ring[0].shape[0], axis=0
+    )
     count = key_piece.shape[0] // BLK
     relative = wanted
     inside = (relative >= 0) & (relative < count)

time: 168 us -> 161 us (0.958)
  blocking collectives: 39 us -> 20.4 us
  waiting for transfers between devices: 17.9 us -> 30 us
  local copies, waits for them, and re-layouts: 37.2 us -> 33.7 us
  starting transfers between devices: 7.61 us -> 10.5 us
    all_gather x1 -> x0, blocking collectives: 16.6 us -> none  [per_device(): value_piece = lax.all_gather(values, 'seq', axis=0, tiled=True)]
    ppermute x0 -> x3, waiting for transfers between devices: none -> 12.1 us  [per_device(): lax.ppermute(ring[-1], 'seq', [(dev, (dev + 1) % 4) for dev in range(4)])]
    broadcast_in_dim x4, local copies, waits for them, and re-layouts: 3.66 us -> 0.05 us  [attend(): weights = jnp.where(mask_heads, jnp.exp(scores - highest), 0.0)]
    ppermute x0 -> x3, starting transfers between devices: none -> 3.51 us  [per_device(): lax.ppermute(ring[-1], 'seq', [(dev, (dev + 1) % 4) for dev in range(4)])]
    all_gather x1, blocking collectives: 17.6 us -> 15.6 us  [per_device(): key_piece = lax.all_gather(keys, 'seq', axis=0, tiled=True)]
  transfers between devices with their start and end apart: 2 -> 5, of which waited for: 2 -> 4; matrix products, arithmetic and copies ran while one was open for 2% -> 5% of each run, Pallas kernels for 0% -> 0%
where the time goes in v1:
time: 161 us; the launch traced here: 160 us
  matrix products  36.2 us (22%)
  local copies, waits for them, and re-layouts  33.7 us (21%)
  waiting for transfers between devices  30 us (19%)
  other arithmetic  27.7 us (17%)
  blocking collectives  20.4 us (13%)
  starting transfers between devices  10.5 us (7%)
    all_gather x1, blocking collectives, per_device(): key_piece = lax.all_gather(keys, 'seq', axis=0, tiled=True)  15.6 us
    ppermute x3, waiting for transfers between devices, per_device(): lax.ppermute(ring[-1], 'seq', [(dev, (dev + 1) % 4) for dev in range(4)])  12.1 us
    dot_general x4, matrix products, attend(): jnp.einsum('qigw,qsw->qgis', do_group, v_group, preferred_element_type=jn...  9.67 us
    all_to_all x1, waiting for transfers between devices, per_device(): lax.all_to_all(send_value_tiles, 'seq', split_axis=0, concat_axis=0, tile...  9 us
    all_to_all x1, waiting for transfers between devices, per_device(): lax.all_to_all(send_key_tiles, 'seq', split_axis=0, concat_axis=0, tiled=...  8.89 us
    scatter-add x4, other arithmetic, attend(): value_acc.at[rows_group].add(value_terms.reshape(group * TOPK, BLK * width))  8.42 us
    scatter-add x4, other arithmetic, attend(): key_acc.at[rows_group].add(key_terms.reshape(group * TOPK, BLK * width))  8.42 us
    dot_general x4, matrix products, attend(): jnp.einsum('qgis,qigw->qsw', probs_b, do_group, preferred_element_type=jn...  6.69 us
  transfers between devices with their start and end apart: 5, of which 4 were waited for; matrix products, arithmetic and copies ran while one was open for 5% of the time, Pallas kernels for 0%

profile of v1, /device:TPU:0, one launch (start us, length us, event | category | flops | bytes accessed | tf_op | source)
XLA Modules:
  0.0 159.8 jit_solution(7180185238645311445)
XLA Ops:
  0.6 3.1 %collective-permute-start = (bf16[512,1,128]{2,0,1:T(8,128)(2,1)}, bf16[512,1,128]{2,0,1:T(8,128)(2,1)S(1)}, u32[]{:S(2)}, u32[]{:S(2)}) collective-permute-start(bf16[512,1,128]{2,0,1:T(8,128)(2,1)} %param.13), channel_id=1, source_target_pairs={{0,4},{4,8},{8,12},{12,0},{1,5},{5,9},{9,13},{13,1},{2,6},{6,10},{... | collective-permute-start | bytes 393224 | tf_op jit(solution)/shard_map/ppermute | solution.py:54
  6.4 15.6 %all_gather.3 = bf16[2048,1,128]{2,0,1:T(8,128)(2,1)S(1)} all-gather(bf16[512,1,128]{2,0,1:T(8,128)(2,1)} %param.12), channel_id=1, replica_groups=mesh['groups'=2,'seq'=4,'head'=2,'inner'=2] {'seq'}, dimensions={0}, use_global_device_ids=true | all-gather | bytes 655360 | tf_op jit(solution)/shard_map/all_gather | solution.py:51
  24.8 6.0 %collective-permute-done.1 = bf16[512,1,128]{2,0,1:T(8,128)(2,1)S(1)} collective-permute-done((bf16[512,1,128]{2,0,1:T(8,128)(2,1)S(1)}, bf16[512,1,128]{2,0,1:T(8,128)(2,1)S(1)}, u32[]{:S(2)}, u32[]{:S(2)}) %collective-permute-start.1) | collective-permute-done | bytes 131104 | tf_op jit(solution)/shard_map/ppermute | solution.py:54
  31.5 6.1 %collective-permute-done.2 = bf16[512,1,128]{2,0,1:T(8,128)(2,1)S(1)} collective-permute-done((bf16[512,1,128]{2,0,1:T(8,128)(2,1)S(1)}, bf16[512,1,128]{2,0,1:T(8,128)(2,1)S(1)}, u32[]{:S(2)}, u32[]{:S(2)}) %collective-permute-start.2) | collective-permute-done | bytes 131104 | tf_op jit(solution)/shard_map/ppermute | solution.py:54
  37.8 2.1 %gather_fusion.1 = bf16[128,64,128]{2,1,0:T(8,128)(2,1)} fusion(bf16[32,64,128]{2,1,0:T(8,128)(2,1)S(1)} %bitcast.132, s32[1024]{0:T(1024)S(1)} %pad_clamp_fusion), kind=kCustom, calls=%fused_computation.1.clone | custom fusion | bytes 4194816 | tf_op jit(solution)/shard_map/jit(_take)/gather | solution.py:63
  40.0 3.7 %select_select_fusion = (bf16[128,64,128]{2,1,0:T(8,128)(2,1)}, bf16[128,64,128]{2,1,0:T(8,128)(2,1)}) fusion(bf16[128,64,128]{2,1,0:T(8,128)(2,1)} %gather_fusion.1, pred[128]{0:T(512)(128)(4,1)S(1)} %compare_and_fusion.2, pred[128]{0:T(512)(128)(4,1)S(1)} %and.172, bf16[128,64,128]{2,1,0:T(8,128)(2,1)S(1)} %gather_fusion), kind=kLoop, calls=%fused_computation.54 | loop fusion | flops 4194304 | bytes 8388864 | tf_op jit(solution)/shard_map/jit(_where)/select_n | solution.py:65
  43.8 80.4 %while.14 = (s32[]{:T(128)}, f32[24,8192]{1,0:T(8,128)S(1)}, f32[24,8192]{1,0:T(8,128)S(1)}, bf16[4,2,64,4,128]{4,3,2,1,0:T(4,128)(2,1)}, s32[4,32]{1,0:T(4,128)...) while((s32[]{:T(128)}, f32[24,8192]{1,0:T(8,128)S(1)}, ...), condition=%wide.region_9.11_spmd, body=%wide.region_3.10_spmd.sunk | while | flops 679871104 | bytes 52703944 | solution.py:115
  44.9 1.5 fusion.74
  48.6 1.7 %convolution_bitcast_fusion.5 = f32[2,1024,128]{2,1,0:T(8,128)} fusion(bf16[1,2,64,4,128]{4,3,2,1,0:T(4,128)(2,1)S(1)} %get-tuple-element.196, f32[2,4,64,1024]{3,2,1,0:T(8,128)S(1)} %get-tuple-element.194, f32[2,4,64]{2,1,0:T(4,128)S(1)} %get-tuple-element.195), kind=kOutput, calls=%fused_computation.16.clone.1 | convolution fusion | flops 135266304 | bytes 3278848 | tf_op jit(solution)/shard_map/while/body/eval_jaxpr/qgis,qigw->qsw/dot_general | solution.py:107
  50.2 1.4 reshape.340
  51.6 2.1 %scatter_fusion.1 = f32[24,8192]{1,0:T(8,128)S(1)} fusion(f32[24,8192]{1,0:T(8,128)S(1)} %get-tuple-element.212, s32[32]{0:T(128)S(1)} %fusion.73, f32[32,8192]{1,0:T(8,128)S(1)} %reshape.340), kind=kCustom, calls=%fused_computation.3.clone.1 | custom fusion | flops 262144 | bytes 3145856 | tf_op jit(solution)/shard_map/while/body/eval_jaxpr/scatter-add | solution.py:111
  53.8 2.4 %fusion.76 = (f32[2,4,64]{2,1,0:T(4,128)S(1)}, f32[2,1024,64,4]{1,2,3,0:T(8,128)S(1)}) fusion(f32[2,4,64,1024]{3,2,1,0:T(8,128)} %copy-done, f32[2,4,64]{2,1,0:T(4,128)S(1)} %get-tuple-element.195, bf16[1,2,64,4,128]{4,3,2,1,0:T(4,128)(2,1)S(1)} %get-tuple-element.196, bf16[4,2,1024,128]{3,2,1,0:T(8,128)(2,1)} %get-tuple-element.229, s32[]{:T(128)S(6)} %copy.91), kind=kOutput, calls=%fused_computation.7.clone.1 | convolution fusion | flops 135790080 | bytes 4853764 | tf_op jit(solution)/shard_map/while/body/eval_jaxpr/qigw,qsw->qgis/dot_general | solution.py:96
  56.6 1.5 fusion.79
  58.1 1.5 fusion.78
  59.6 1.4 reshape.339
  61.0 2.1 %scatter_fusion = f32[24,8192]{1,0:T(8,128)S(1)} fusion(f32[24,8192]{1,0:T(8,128)S(1)} %get-tuple-element.211, s32[32]{0:T(128)S(1)} %fusion.73, f32[32,8192]{1,0:T(8,128)S(1)} %reshape.339), kind=kCustom, calls=%fused_computation.2.clone.1 | custom fusion | flops 262144 | bytes 3145856 | tf_op jit(solution)/shard_map/while/body/eval_jaxpr/scatter-add | solution.py:110
  65.0 1.5 fusion.74
  68.6 1.7 %convolution_bitcast_fusion.5 = f32[2,1024,128]{2,1,0:T(8,128)} fusion(bf16[1,2,64,4,128]{4,3,2,1,0:T(4,128)(2,1)S(1)} %get-tuple-element.196, f32[2,4,64,1024]{3,2,1,0:T(8,128)S(1)} %get-tuple-element.194, f32[2,4,64]{2,1,0:T(4,128)S(1)} %get-tuple-element.195), kind=kOutput, calls=%fused_computation.16.clone.1 | convolution fusion | flops 135266304 | bytes 3278848 | tf_op jit(solution)/shard_map/while/body/eval_jaxpr/qgis,qigw->qsw/dot_general | solution.py:107
  70.3 1.4 reshape.340
  71.7 2.1 %scatter_fusion.1 = f32[24,8192]{1,0:T(8,128)S(1)} fusion(f32[24,8192]{1,0:T(8,128)S(1)} %get-tuple-element.212, s32[32]{0:T(128)S(1)} %fusion.73, f32[32,8192]{1,0:T(8,128)S(1)} %reshape.340), kind=kCustom, calls=%fused_computation.3.clone.1 | custom fusion | flops 262144 | bytes 3145856 | tf_op jit(solution)/shard_map/while/body/eval_jaxpr/scatter-add | solution.py:111
  73.9 2.4 %fusion.76 = (f32[2,4,64]{2,1,0:T(4,128)S(1)}, f32[2,1024,64,4]{1,2,3,0:T(8,128)S(1)}) fusion(f32[2,4,64,1024]{3,2,1,0:T(8,128)} %copy-done, f32[2,4,64]{2,1,0:T(4,128)S(1)} %get-tuple-element.195, bf16[1,2,64,4,128]{4,3,2,1,0:T(4,128)(2,1)S(1)} %get-tuple-element.196, bf16[4,2,1024,128]{3,2,1,0:T(8,128)(2,1)} %get-tuple-element.229, s32[]{:T(128)S(6)} %copy.91), kind=kOutput, calls=%fused_computation.7.clone.1 | convolution fusion | flops 135790080 | bytes 4853764 | tf_op jit(solution)/shard_map/while/body/eval_jaxpr/qigw,qsw->qgis/dot_general | solution.py:96
  76.7 1.5 fusion.79
  78.1 1.5 fusion.78
  79.7 1.4 reshape.339
  81.1 2.1 %scatter_fusion = f32[24,8192]{1,0:T(8,128)S(1)} fusion(f32[24,8192]{1,0:T(8,128)S(1)} %get-tuple-element.211, s32[32]{0:T(128)S(1)} %fusion.73, f32[32,8192]{1,0:T(8,128)S(1)} %reshape.339), kind=kCustom, calls=%fused_computation.2.clone.1 | custom fusion | flops 262144 | bytes 3145856 | tf_op jit(solution)/shard_map/while/body/eval_jaxpr/scatter-add | solution.py:110
  85.1 1.5 fusion.74
  88.7 1.7 %convolution_bitcast_fusion.5 = f32[2,1024,128]{2,1,0:T(8,128)} fusion(bf16[1,2,64,4,128]{4,3,2,1,0:T(4,128)(2,1)S(1)} %get-tuple-element.196, f32[2,4,64,1024]{3,2,1,0:T(8,128)S(1)} %get-tuple-element.194, f32[2,4,64]{2,1,0:T(4,128)S(1)} %get-tuple-element.195), kind=kOutput, calls=%fused_computation.16.clone.1 | convolution fusion | flops 135266304 | bytes 3278848 | tf_op jit(solution)/shard_map/while/body/eval_jaxpr/qgis,qigw->qsw/dot_general | solution.py:107
  90.4 1.4 reshape.340
  91.8 2.1 %scatter_fusion.1 = f32[24,8192]{1,0:T(8,128)S(1)} fusion(f32[24,8192]{1,0:T(8,128)S(1)} %get-tuple-element.212, s32[32]{0:T(128)S(1)} %fusion.73, f32[32,8192]{1,0:T(8,128)S(1)} %reshape.340), kind=kCustom, calls=%fused_computation.3.clone.1 | custom fusion | flops 262144 | bytes 3145856 | tf_op jit(solution)/shard_map/while/body/eval_jaxpr/scatter-add | solution.py:111
  93.9 2.4 %fusion.76 = (f32[2,4,64]{2,1,0:T(4,128)S(1)}, f32[2,1024,64,4]{1,2,3,0:T(8,128)S(1)}) fusion(f32[2,4,64,1024]{3,2,1,0:T(8,128)} %copy-done, f32[2,4,64]{2,1,0:T(4,128)S(1)} %get-tuple-element.195, bf16[1,2,64,4,128]{4,3,2,1,0:T(4,128)(2,1)S(1)} %get-tuple-element.196, bf16[4,2,1024,128]{3,2,1,0:T(8,128)(2,1)} %get-tuple-element.229, s32[]{:T(128)S(6)} %copy.91), kind=kOutput, calls=%fused_computation.7.clone.1 | convolution fusion | flops 135790080 | bytes 4853764 | tf_op jit(solution)/shard_map/while/body/eval_jaxpr/qigw,qsw->qgis/dot_general | solution.py:96
  96.7 1.5 fusion.79
  98.2 1.5 fusion.78
  99.8 1.4 reshape.339
  101.2 2.1 %scatter_fusion = f32[24,8192]{1,0:T(8,128)S(1)} fusion(f32[24,8192]{1,0:T(8,128)S(1)} %get-tuple-element.211, s32[32]{0:T(128)S(1)} %fusion.73, f32[32,8192]{1,0:T(8,128)S(1)} %reshape.339), kind=kCustom, calls=%fused_computation.2.clone.1 | custom fusion | flops 262144 | bytes 3145856 | tf_op jit(solution)/shard_map/while/body/eval_jaxpr/scatter-add | solution.py:110
  105.2 1.5 fusion.74
  108.8 1.7 %convolution_bitcast_fusion.5 = f32[2,1024,128]{2,1,0:T(8,128)} fusion(bf16[1,2,64,4,128]{4,3,2,1,0:T(4,128)(2,1)S(1)} %get-tuple-element.196, f32[2,4,64,1024]{3,2,1,0:T(8,128)S(1)} %get-tuple-element.194, f32[2,4,64]{2,1,0:T(4,128)S(1)} %get-tuple-element.195), kind=kOutput, calls=%fused_computation.16.clone.1 | convolution fusion | flops 135266304 | bytes 3278848 | tf_op jit(solution)/shard_map/while/body/eval_jaxpr/qgis,qigw->qsw/dot_general | solution.py:107
  110.5 1.4 reshape.340
  111.9 2.1 %scatter_fusion.1 = f32[24,8192]{1,0:T(8,128)S(1)} fusion(f32[24,8192]{1,0:T(8,128)S(1)} %get-tuple-element.212, s32[32]{0:T(128)S(1)} %fusion.73, f32[32,8192]{1,0:T(8,128)S(1)} %reshape.340), kind=kCustom, calls=%fused_computation.3.clone.1 | custom fusion | flops 262144 | bytes 3145856 | tf_op jit(solution)/shard_map/while/body/eval_jaxpr/scatter-add | solution.py:111
  114.0 2.4 %fusion.76 = (f32[2,4,64]{2,1,0:T(4,128)S(1)}, f32[2,1024,64,4]{1,2,3,0:T(8,128)S(1)}) fusion(f32[2,4,64,1024]{3,2,1,0:T(8,128)} %copy-done, f32[2,4,64]{2,1,0:T(4,128)S(1)} %get-tuple-element.195, bf16[1,2,64,4,128]{4,3,2,1,0:T(4,128)(2,1)S(1)} %get-tuple-element.196, bf16[4,2,1024,128]{3,2,1,0:T(8,128)(2,1)} %get-tuple-element.229, s32[]{:T(128)S(6)} %copy.91), kind=kOutput, calls=%fused_computation.7.clone.1 | convolution fusion | flops 135790080 | bytes 4853764 | tf_op jit(solution)/shard_map/while/body/eval_jaxpr/qigw,qsw->qgis/dot_general | solution.py:96
  116.8 1.5 fusion.79
  118.3 1.5 fusion.78
  119.9 1.4 reshape.339
  121.3 2.1 %scatter_fusion = f32[24,8192]{1,0:T(8,128)S(1)} fusion(f32[24,8192]{1,0:T(8,128)S(1)} %get-tuple-element.211, s32[32]{0:T(128)S(1)} %fusion.73, f32[32,8192]{1,0:T(8,128)S(1)} %reshape.339), kind=kCustom, calls=%fused_computation.2.clone.1 | custom fusion | flops 262144 | bytes 3145856 | tf_op jit(solution)/shard_map/while/body/eval_jaxpr/scatter-add | solution.py:110
  125.1 3.5 %all-to-all-start = ((f32[4,4,8192]{2,1,0:T(4,128)}), f32[4,4,8192]{2,1,0:T(4,128)S(1)}, u32[]{:S(2)}, u32[]{:S(2)}) async-start(f32[4,4,8192]{2,1,0:T(4,128)} %reshape.280), calls=%async_computation | async-start | bytes 1048576 | tf_op jit(solution)/shard_map/all_to_all | solution.py:127
  130.0 8.9 %all-to-all-done = f32[4,4,8192]{2,1,0:T(4,128)S(1)} async-done(((f32[4,4,8192]{2,1,0:T(4,128)}), f32[4,4,8192]{2,1,0:T(4,128)S(1)}, u32[]{:S(2)}, u32[]{:S(2)}) %all-to-all-start) | async-done | bytes 524320 | tf_op jit(solution)/shard_map/all_to_all | solution.py:127
  138.9 3.5 %all-to-all-start.1 = ((f32[4,4,8192]{2,1,0:T(4,128)}), f32[4,4,8192]{2,1,0:T(4,128)S(1)}, u32[]{:S(2)}, u32[]{:S(2)}) async-start(f32[4,4,8192]{2,1,0:T(4,128)} %reshape.282), calls=%async_computation.1 | async-start | bytes 1048576 | tf_op jit(solution)/shard_map/all_to_all | solution.py:128
  143.6 9.0 %all-to-all-done.1 = f32[4,4,8192]{2,1,0:T(4,128)S(1)} async-done(((f32[4,4,8192]{2,1,0:T(4,128)}), f32[4,4,8192]{2,1,0:T(4,128)S(1)}, u32[]{:S(2)}, u32[]{:S(2)}) %all-to-all-start.1) | async-done | bytes 524320 | tf_op jit(solution)/shard_map/all_to_all | solution.py:128
  153.5 4.8 %all-reduce.2 = (bf16[8,8192]{1,0:T(8,128)(2,1)S(1)}, bf16[8,8192]{1,0:T(8,128)(2,1)S(1)}) all-reduce(f32[8,8192]{1,0:T(8,128)S(1)} %fusion.30, f32[8,8192]{1,0:T(8,128)S(1)} %fusion.31), channel_id=1, replica_groups=mesh['groups'=2,'seq'=4,'head'=2,'inner'=2] {'inner'}, use_global_device_ids=true, to_apply=%region_12.14 | all-reduce | flops 131072 | bytes 786432 | tf_op jit(solution)/shard_map/psum | solution.py:136
  (111 shorter events, 29.7 us)
Async XLA Ops:
  0.6 23.3 %collective-permute-start = (bf16[512,1,128]{2,0,1:T(8,128)(2,1)}, bf16[512,1,128]{2,0,1:T(8,128)(2,1)S(1)}, u32[]{:S(2)}, u32[]{:S(2)}) collective-permute-start(bf16[512,1,128]{2,0,1:T(8,128)(2,1)} %param.13), channel_id=1, source_target_pairs={{0,4},{4,8},{8,12},{12,0},{1,5},{5,9},{9,13},{13,1},{2,6},{6,10},{... | collective-permute-start | bytes 393224 | tf_op jit(solution)/shard_map/ppermute | solution.py:54
  4.7 0.8 copy-start.3
  23.0 14.6 %copy-start.2 = (bf16[512,1,128]{2,0,1:T(8,128)(2,1)S(1)}, bf16[512,1,128]{2,0,1:T(8,128)(2,1)}, u32[]{:S(2)}) copy-start(bf16[512,1,128]{2,0,1:T(8,128)(2,1)} %param.13) | copy-start | bytes 393220
  24.0 6.8 %collective-permute-start.1 = (bf16[512,1,128]{2,0,1:T(8,128)(2,1)S(1)}, bf16[512,1,128]{2,0,1:T(8,128)(2,1)S(1)}, u32[]{:S(2)}, u32[]{:S(2)}) collective-permute-start(bf16[512,1,128]{2,0,1:T(8,128)(2,1)S(1)} %collective-permute-done), channel_id=1, source_target_pairs={{0,4},{4,8},{8,12},{12,0},{1,5},{5,9},{9,13},{13,1},{2,6},{6,10},{... | collective-permute-start | bytes 393224 | tf_op jit(solution)/shard_map/ppermute | solution.py:54
  30.8 6.8 %collective-permute-start.2 = (bf16[512,1,128]{2,0,1:T(8,128)(2,1)S(1)}, bf16[512,1,128]{2,0,1:T(8,128)(2,1)S(1)}, u32[]{:S(2)}, u32[]{:S(2)}) collective-permute-start(bf16[512,1,128]{2,0,1:T(8,128)(2,1)S(1)} %collective-permute-done.1), channel_id=1, source_target_pairs={{0,4},{4,8},{8,12},{12,0},{1,5},{5,9},{9,13},{13,1},{2,6},{6,10},{... | collective-permute-start | bytes 393224 | tf_op jit(solution)/shard_map/ppermute | solution.py:54
  47.3 1.3 copy-start
  53.8 2.4 %copy-start.1 = (f32[2,4,64,1024]{3,2,1,0:T(8,128)S(1)}, f32[2,4,64,1024]{3,2,1,0:T(8,128)}, u32[]{:S(2)}) copy-start(f32[2,4,64,1024]{3,2,1,0:T(8,128)} %copy-done) | copy-start | bytes 6291460 | tf_op jit(solution)/shard_map/while
  67.3 1.3 copy-start
  73.8 2.4 %copy-start.1 = (f32[2,4,64,1024]{3,2,1,0:T(8,128)S(1)}, f32[2,4,64,1024]{3,2,1,0:T(8,128)}, u32[]{:S(2)}) copy-start(f32[2,4,64,1024]{3,2,1,0:T(8,128)} %copy-done) | copy-start | bytes 6291460 | tf_op jit(solution)/shard_map/while
  87.4 1.3 copy-start
  93.9 2.4 %copy-start.1 = (f32[2,4,64,1024]{3,2,1,0:T(8,128)S(1)}, f32[2,4,64,1024]{3,2,1,0:T(8,128)}, u32[]{:S(2)}) copy-start(f32[2,4,64,1024]{3,2,1,0:T(8,128)} %copy-done) | copy-start | bytes 6291460 | tf_op jit(solution)/shard_map/while
  107.5 1.3 copy-start
  114.0 2.4 %copy-start.1 = (f32[2,4,64,1024]{3,2,1,0:T(8,128)S(1)}, f32[2,4,64,1024]{3,2,1,0:T(8,128)}, u32[]{:S(2)}) copy-start(f32[2,4,64,1024]{3,2,1,0:T(8,128)} %copy-done) | copy-start | bytes 6291460 | tf_op jit(solution)/shard_map/while
  125.1 13.7 %all-to-all-start = ((f32[4,4,8192]{2,1,0:T(4,128)}), f32[4,4,8192]{2,1,0:T(4,128)S(1)}, u32[]{:S(2)}, u32[]{:S(2)}) async-start(f32[4,4,8192]{2,1,0:T(4,128)} %reshape.280), calls=%async_computation | async-start | bytes 1048576 | tf_op jit(solution)/shard_map/all_to_all | solution.py:127
  138.9 13.7 %all-to-all-start.1 = ((f32[4,4,8192]{2,1,0:T(4,128)}), f32[4,4,8192]{2,1,0:T(4,128)S(1)}, u32[]{:S(2)}, u32[]{:S(2)}) async-start(f32[4,4,8192]{2,1,0:T(4,128)} %reshape.282), calls=%async_computation.1 | async-start | bytes 1048576 | tf_op jit(solution)/shard_map/all_to_all | solution.py:128
